TPU v7x, 512 devices: a whole 4x4x16 slice. The times are simulated.
512 devices in a mesh: gx: 4 (over z_hi), gy: 8 (over y, core), gz: 16 (over x, z_lo).
Axes of the slice: x: 4, y: 4, z: 16 (z_hi: 4, z_lo: 4; z = z_hi * 4 + z_lo), core: 2. Of those that a mesh axis runs over, the one named last changes fastest.
Arguments:
- right_side: float32 [4, 8, 16, 6, 1024], P('gx', 'gy', 'gz'), may hold values from -18 to 18
- grain_diag: float32 [4, 8, 16, 6, 1024], P('gx', 'gy', 'gz'), may hold values from 0.05 to 0.5
- stiffness: float32 [4, 4], replicated, may hold values from 0.3 to 3
- contact_own: int32 [4, 8, 16, 3072], P('gx', 'gy', 'gz'), may hold values from 0 to 1023, as said below
- contact_slot: int32 [4, 8, 16, 3072], P('gx', 'gy', 'gz'), may hold values from 0 to 7679, as said below
- contact_type: int32 [4, 8, 16, 3072], P('gx', 'gy', 'gz'), may hold values from 0 to 4, as said below
- contact_normal: float32 [4, 8, 16, 3, 3072], P('gx', 'gy', 'gz'), may hold values from -1 to 1, as said below
- contact_radii: float32 [4, 8, 16, 2, 3072], P('gx', 'gy', 'gz'), may hold values from 0.4 to 1
Outputs:
- solution_field: float32 [4, 8, 16, 6, 1024], P('gx', 'gy', 'gz')
- residual: float32 [4, 8, 16, 6, 1024], P('gx', 'gy', 'gz')
Inputs may be any that keep to these rules, and one draw needn't show every extreme that they name: `contact_normal`: each normal has unit length. `contact_own`: in the first 2240 slots of a block the own grain differs from the partner; in the last 832 slots the own grain is one of the block's first 256 grains. `contact_slot`: the first 2240 slots of a block hold values below 1024; the slots 3072 - 832 + k * 32 to 2240 + (k + 1) * 32 - 1, for k = 0 to 25, hold values from 1024 + k * 256 to 1024 + (k + 1) * 256 - 1. `contact_type`: the value 4 marks an empty slot.
All inputs are finite; a program needn't handle non-finite values.
Results may differ from a plain program's by a relative error of at most 0.00018.
Values sent between devices are 32-bit elements; how exact they have to be, the bound alone decides.
A program may use at most 64 MiB of HBM per device.

v0:
```python
import jax
import jax.numpy as jnp
import numpy as np
from jax import lax
from jax.sharding import Mesh
from jax.sharding import PartitionSpec as P

ITERS = 4
GX_GY_GZ = ("gx", "gy_0", "gy_1", "gz_0", "gz_1")
GY = ("gy_0", "gy_1")
GZ = ("gz_0", "gz_1")


def one_axis_at_a_time(value, axes):
    for axis in axes:
        value = lax.psum(value, axis)
    return value


def with_halo(block, sides, width):
    for axis, dim in sides:
        count = lax.axis_size(axis)
        forward = [(i, i + 1) for i in range(count - 1)]
        forward.append((count - 1, 0))
        backward = [(target, source) for source, target in forward]
        low = lax.ppermute(
            lax.slice_in_dim(block, block.shape[dim] - width, None, axis=dim), axis, forward
        )
        high = lax.ppermute(lax.slice_in_dim(block, 0, width, axis=dim), axis, backward)
        block = jnp.concatenate([low, block, high], axis=dim)
    return block


def cross(left, right):
    return jnp.stack(
        [
            left[1] * right[2] - left[2] * right[1],
            left[2] * right[0] - left[0] * right[2],
            left[0] * right[1] - left[1] * right[0],
        ]
    )


def lookup(stiffness, ctype):
    total = jnp.zeros((4,) + ctype.shape, stiffness.dtype)
    for which in range(stiffness.shape[1]):
        total = total + stiffness[:, which : which + 1] * (ctype == which)[None].astype(
            stiffness.dtype
        )
    return total


def contact_response(first_u, second_u, normal, radii, coeff):
    normal_k, shear_k, roll_k, twist_k = (coeff[0], coeff[1], coeff[2], coeff[3])
    first_r, second_r = (radii[0], radii[1])
    delta = (
        second_u[:3]
        - second_r * cross(second_u[3:], normal)
        - first_u[:3]
        - first_r * cross(first_u[3:], normal)
    )
    along = jnp.sum(normal * delta, axis=0)
    force = shear_k * delta + (normal_k - shear_k) * along * normal
    theta = second_u[3:] - first_u[3:]
    twist = jnp.sum(normal * theta, axis=0)
    moment = roll_k * theta + (twist_k - roll_k) * twist * normal
    lever = cross(normal, force)
    on_first = jnp.concatenate([force, first_r * lever + moment], axis=0)
    on_second = jnp.concatenate([-force, second_r * lever - moment], axis=0)
    return (on_first, on_second)


def full_position(block):
    return block + (block >= 13).astype(jnp.int32)


def paired(residual, image):
    return (
        one_axis_at_a_time(jnp.sum(residual * residual), GX_GY_GZ),
        one_axis_at_a_time(jnp.sum(residual * image), GX_GY_GZ),
    )


def shards(
    right_side,
    grain_diag,
    stiffness,
    contact_own,
    contact_slot,
    contact_type,
    contact_normal,
    contact_radii,
):
    rhs = right_side[0, 0, 0]
    diag = grain_diag[0, 0, 0]
    grains = rhs.shape[1]
    rim = grains // 4
    owners = contact_own[0, 0, 0]
    slots = contact_slot[0, 0, 0]
    ctype = contact_type[0, 0, 0]
    normal = contact_normal[0, 0, 0]
    radii = contact_radii[0, 0, 0]
    coeff = lookup(stiffness, ctype)
    far_slot = slots >= grains
    rel = jnp.maximum(slots - grains, 0)
    ghost_column = full_position(rel // rim) * rim + rel % rim
    near_grain = jnp.where(far_slot, 0, slots)
    group_size = grains // 32
    remote_count = 26 * group_size
    packed = jnp.stack([owners[-remote_count:], slots[-remote_count:], ctype[-remote_count:]])[
        None, None, None
    ]
    theirs = with_halo(packed, (("gx", 0), (GY, 1), (GZ, 2)), 1).reshape(27, 3, 26, group_size)
    geometry = jnp.concatenate([normal[:, -remote_count:], radii[:, -remote_count:]], axis=0)[
        None, None, None
    ]
    their_geometry = with_halo(geometry, (("gx", 0), (GY, 1), (GZ, 2)), 1).reshape(
        27, 5, 26, group_size
    )
    counts = (lax.axis_size("gx"), lax.axis_size(GY), lax.axis_size(GZ))
    chosen_place = []
    chosen_group = []
    for place in range(27):
        for group in range(26):
            whole = group + (1 if group >= 13 else 0)
            back_x = (place // 9 - 1 + whole // 9 - 1) % counts[0] == 0
            back_y = (place // 3 % 3 - 1 + whole // 3 % 3 - 1) % counts[1] == 0
            back_z = (place % 3 - 1 + whole % 3 - 1) % counts[2] == 0
            if back_x and back_y and back_z:
                chosen_place.append(place)
                chosen_group.append(group)
    place_index = np.array(chosen_place, np.int32)
    group_index = np.array(chosen_group, np.int32)
    picked = theirs[place_index, :, group_index]
    picked_geometry = their_geometry[place_index, :, group_index]
    mirror_coeff = lookup(stiffness, picked[:, 2].reshape(-1))
    mirror_normal = jnp.moveaxis(picked_geometry[:, :3], 1, 0).reshape(3, -1)
    mirror_radii = jnp.moveaxis(picked_geometry[:, 3:], 1, 0).reshape(2, -1)
    mirror_place = jnp.asarray(np.repeat(place_index, group_size))
    mirror_column = mirror_place * rim + picked[:, 0].reshape(-1)
    mirror_mine = ((picked[:, 1] - grains) % rim).reshape(-1)

    def operate(field):
        rims = with_halo(field[None, None, None, :, :rim], (("gx", 0), (GY, 1), (GZ, 2)), 1)
        rim_flat = jnp.moveaxis(rims.reshape(27, 6, rim), 1, 0).reshape(6, 27 * rim)
        first_u = field[:, owners]
        second_u = jnp.where(far_slot[None], rim_flat[:, ghost_column], field[:, near_grain])
        on_first, on_second = contact_response(first_u, second_u, normal, radii, coeff)
        forces = jnp.zeros_like(field).at[:, owners].add(on_first)
        forces = forces.at[:, near_grain].add(jnp.where(far_slot[None], 0.0, on_second))
        their_u = rim_flat[:, mirror_column]
        unused, onto_mine = contact_response(
            their_u, field[:, mirror_mine], mirror_normal, mirror_radii, mirror_coeff
        )
        forces = forces.at[:, mirror_mine].add(onto_mine)
        return diag * field - forces

    solution_field = jnp.zeros_like(rhs)
    residual = rhs
    image = operate(residual)
    norm_now, product = paired(residual, image)
    alpha = norm_now / product
    direction, along = (residual, image)
    for step in range(ITERS):
        solution_field = solution_field + alpha * direction
        residual = residual - alpha * along
        if step + 1 < ITERS:
            image = operate(residual)
            norm_next, product = paired(residual, image)
            ratio = norm_next / norm_now
            alpha = norm_next / (product - ratio * norm_next / alpha)
            direction = residual + ratio * direction
            along = image + ratio * along
            norm_now = norm_next
    return (solution_field[None, None, None], residual[None, None, None])


def solution(mesh):
    torus = Mesh(
        mesh.devices.reshape(mesh.shape["gx"], 4, 2, 4, 4), ("gx", "gy_0", "gy_1", "gz_0", "gz_1")
    )
    placed = (
        P("gx", GY, GZ, None, None),
        P("gx", GY, GZ, None, None),
        P(),
        P("gx", GY, GZ, None),
        P("gx", GY, GZ, None),
        P("gx", GY, GZ, None),
        P("gx", GY, GZ, None, None),
        P("gx", GY, GZ, None, None),
    )
    return jax.shard_map(
        shards,
        mesh=torus,
        in_specs=placed,
        out_specs=(P("gx", GY, GZ, None, None), P("gx", GY, GZ, None, None)),
        check_vma=False,
    )
```

profile of v0, /device:TPU:8, one launch (start us, length us, event | category | flops | bytes accessed | tf_op | source)
XLA Modules:
  0.0 703.4 jit_solution(7459148122912372510)
XLA Ops:
  2.9 12.7 %collective-permute-start.7 = (s32[1,1,1,3,832]{4,3,2,1,0:T(4,128)S(1)}, s32[1,1,1,3,832]{4,3,2,1,0:T(4,128)S(1)}, u32[]{:S(2)}, u32[]{:S(2)}) collective-permute-start(s32[1,1,1,3,832]{4,3,2,1,0:T(4,128)S(1)} %add_bitcast_fusion.1), channel_id=1, source_target_pairs={{128,0},{256,128},{384,256},{0,384},{129,1},{257,129},{385,257},{1... | collective-permute-start | bytes 29960 | tf_op jit(solution)/shard_map/ppermute | solution.py:29
  102.8 10.1 %gather_fusion = f32[3072,6]{1,0:T(8,128)S(1)} fusion(f32[6,6912]{0,1:T(8,128)} %bitcast.453, s32[3072]{0:T(1024)S(1)} %broadcast_clamp_fusion.2), kind=kCustom, calls=%fused_computation | custom fusion | bytes 159744 | tf_op jit(solution)/shard_map/gather | solution.py:147
  116.2 17.4 %scatter_custom_fusion = f32[6,1024]{0,1:T(8,128)S(1)} fusion(s32[3072]{0:T(1024)S(1)} %bitcast.549, f32[3072,6]{1,0:T(8,128)} %copy.972, f32[]{:T(128)} %constant.32.clone.1), kind=kCustom, calls=%fused_computation.42 | custom fusion | flops 18432 | bytes 25088 | tf_op jit(solution)/shard_map/scatter-add | solution.py:149
  133.6 18.6 %scatter_fusion = f32[6,1024]{0,1:T(8,128)S(1)} fusion(f32[6,1024]{0,1:T(8,128)S(1)} %scatter_custom_fusion, s32[3072]{0:T(1024)S(1)} %bitcast.494, f32[3072,6]{1,0:T(8,128)S(1)} %copy.973), kind=kCustom, calls=%fused_computation.23 | custom fusion | flops 18432 | bytes 233472 | tf_op jit(solution)/shard_map/scatter-add | solution.py:150
  183.0 14.6 %all-reduce.15 = (f32[]{:T(128)}, f32[]{:T(128)}) all-reduce(f32[]{:T(128)} %get-tuple-element.40, f32[]{:T(128)} %get-tuple-element.39), channel_id=1, replica_groups=mesh['gx'=4,'gy_0'=4,'gy_1'=2,'gz_0'=4,'gz_1'=4] {'gx'}, use_global_device_ids=true, to_apply=%region_1.2 | all-reduce | flops 2 | bytes 16 | tf_op jit(solution)/shard_map/psum | solution.py:16
  197.6 10.0 %all-reduce.11 = (f32[]{:T(128)}, f32[]{:T(128)}) all-reduce(f32[]{:T(128)} %get-tuple-element.85, f32[]{:T(128)} %get-tuple-element.86), channel_id=1, replica_groups=mesh['gx'=4,'gy_0'=4,'gy_1'=2,'gz_0'=4,'gz_1'=4] {'gy_0'}, use_global_device_ids=true, to_apply=%region_2.3 | all-reduce | flops 2 | bytes 16 | tf_op jit(solution)/shard_map/psum | solution.py:16
  219.0 15.4 %all-reduce.3 = (f32[]{:T(128)}, f32[]{:T(128)}) all-reduce(f32[]{:T(128)} %get-tuple-element.69, f32[]{:T(128)} %get-tuple-element.70), channel_id=1, replica_groups=mesh['gx'=4,'gy_0'=4,'gy_1'=2,'gz_0'=4,'gz_1'=4] {'gz_1'}, use_global_device_ids=true, to_apply=%region_5.6 | all-reduce | flops 2 | bytes 16 | tf_op jit(solution)/shard_map/psum | solution.py:16
  282.2 10.1 %gather_fusion.7 = f32[3072,6]{1,0:T(8,128)S(1)} fusion(f32[6,6912]{0,1:T(8,128)} %bitcast.458, s32[3072]{0:T(1024)S(1)} %broadcast_clamp_fusion.2), kind=kCustom, calls=%fused_computation.7 | custom fusion | bytes 159744 | tf_op jit(solution)/shard_map/gather | solution.py:147
  294.6 17.0 %scatter_custom_fusion.3 = f32[6,1024]{0,1:T(8,128)S(1)} fusion(s32[3072]{0:T(1024)S(1)} %bitcast.550, f32[3072,6]{1,0:T(8,128)S(1)} %copy.998, f32[]{:T(128)} %constant.32.clone.1), kind=kCustom, calls=%fused_computation.40 | custom fusion | flops 18432 | bytes 24580 | tf_op jit(solution)/shard_map/scatter-add | solution.py:149
  312.2 18.4 %scatter_fusion.2 = f32[6,1024]{0,1:T(8,128)S(1)} fusion(f32[6,1024]{0,1:T(8,128)S(1)} %scatter_custom_fusion.3, s32[3072]{0:T(1024)S(1)} %bitcast.495, f32[3072,6]{1,0:T(8,128)S(1)} %copy.999), kind=kCustom, calls=%fused_computation.26 | custom fusion | flops 18432 | bytes 233472 | tf_op jit(solution)/shard_map/scatter-add | solution.py:150
  337.7 14.7 %all-reduce.14 = (f32[]{:T(128)}, f32[]{:T(128)}) all-reduce(f32[]{:T(128)} %get-tuple-element.36, f32[]{:T(128)} %get-tuple-element.35), channel_id=1, replica_groups=mesh['gx'=4,'gy_0'=4,'gy_1'=2,'gz_0'=4,'gz_1'=4] {'gx'}, use_global_device_ids=true, to_apply=%region_20.21 | all-reduce | flops 2 | bytes 16 | tf_op jit(solution)/shard_map/psum | solution.py:16
  352.4 10.2 %all-reduce.10 = (f32[]{:T(128)}, f32[]{:T(128)}) all-reduce(f32[]{:T(128)} %get-tuple-element.83, f32[]{:T(128)} %get-tuple-element.84), channel_id=1, replica_groups=mesh['gx'=4,'gy_0'=4,'gy_1'=2,'gz_0'=4,'gz_1'=4] {'gy_0'}, use_global_device_ids=true, to_apply=%region_21.22 | all-reduce | flops 2 | bytes 16 | tf_op jit(solution)/shard_map/psum | solution.py:16
  374.2 13.5 %all-reduce.2 = (f32[]{:T(128)}, f32[]{:T(128)}) all-reduce(f32[]{:T(128)} %get-tuple-element.67, f32[]{:T(128)} %get-tuple-element.68), channel_id=1, replica_groups=mesh['gx'=4,'gy_0'=4,'gy_1'=2,'gz_0'=4,'gz_1'=4] {'gz_1'}, use_global_device_ids=true, to_apply=%region_24.25 | all-reduce | flops 2 | bytes 16 | tf_op jit(solution)/shard_map/psum | solution.py:16
  438.8 10.1 %gather_fusion.12 = f32[3072,6]{1,0:T(8,128)S(1)} fusion(f32[6,6912]{0,1:T(8,128)} %bitcast.460, s32[3072]{0:T(1024)S(1)} %broadcast_clamp_fusion.2), kind=kCustom, calls=%fused_computation.12 | custom fusion | bytes 159744 | tf_op jit(solution)/shard_map/gather | solution.py:147
  451.1 17.0 %scatter_custom_fusion.6 = f32[6,1024]{0,1:T(8,128)S(1)} fusion(s32[3072]{0:T(1024)S(1)} %bitcast.551, f32[3072,6]{1,0:T(8,128)S(1)} %copy.1017, f32[]{:T(128)} %constant.32.clone.1), kind=kCustom, calls=%fused_computation.38 | custom fusion | flops 18432 | bytes 24580 | tf_op jit(solution)/shard_map/scatter-add | solution.py:149
  468.7 18.4 %scatter_fusion.4 = f32[6,1024]{0,1:T(8,128)S(1)} fusion(f32[6,1024]{0,1:T(8,128)S(1)} %scatter_custom_fusion.6, s32[3072]{0:T(1024)S(1)} %bitcast.496, f32[3072,6]{1,0:T(8,128)S(1)} %copy.1018), kind=kCustom, calls=%fused_computation.29 | custom fusion | flops 18432 | bytes 233472 | tf_op jit(solution)/shard_map/scatter-add | solution.py:150
  494.2 14.6 %all-reduce.13 = (f32[]{:T(128)}, f32[]{:T(128)}) all-reduce(f32[]{:T(128)} %get-tuple-element.34, f32[]{:T(128)} %get-tuple-element.33), channel_id=1, replica_groups=mesh['gx'=4,'gy_0'=4,'gy_1'=2,'gz_0'=4,'gz_1'=4] {'gx'}, use_global_device_ids=true, to_apply=%region_39.40 | all-reduce | flops 2 | bytes 16 | tf_op jit(solution)/shard_map/psum | solution.py:16
  528.9 13.4 %all-reduce.1 = (f32[]{:T(128)}, f32[]{:T(128)}) all-reduce(f32[]{:T(128)} %get-tuple-element.65, f32[]{:T(128)} %get-tuple-element.66), channel_id=1, replica_groups=mesh['gx'=4,'gy_0'=4,'gy_1'=2,'gz_0'=4,'gz_1'=4] {'gz_1'}, use_global_device_ids=true, to_apply=%region_43.44 | all-reduce | flops 2 | bytes 16 | tf_op jit(solution)/shard_map/psum | solution.py:16
  592.5 10.1 %gather_fusion.17 = f32[3072,6]{1,0:T(8,128)S(1)} fusion(f32[6,6912]{0,1:T(8,128)} %bitcast.456, s32[3072]{0:T(1024)S(1)} %broadcast_clamp_fusion.2), kind=kCustom, calls=%fused_computation.17 | custom fusion | bytes 159744 | tf_op jit(solution)/shard_map/gather | solution.py:147
  604.8 17.0 %scatter_custom_fusion.9 = f32[6,1024]{0,1:T(8,128)S(1)} fusion(s32[3072]{0:T(1024)S(1)} %bitcast.552, f32[3072,6]{1,0:T(8,128)S(1)} %copy.1036, f32[]{:T(128)} %constant.32.clone.1), kind=kCustom, calls=%fused_computation.36 | custom fusion | flops 18432 | bytes 24580 | tf_op jit(solution)/shard_map/scatter-add | solution.py:149
  622.4 18.4 %scatter_fusion.6 = f32[6,1024]{0,1:T(8,128)S(1)} fusion(f32[6,1024]{0,1:T(8,128)S(1)} %scatter_custom_fusion.9, s32[3072]{0:T(1024)S(1)} %bitcast.497, f32[3072,6]{1,0:T(8,128)S(1)} %copy.1037), kind=kCustom, calls=%fused_computation.32 | custom fusion | flops 18432 | bytes 233472 | tf_op jit(solution)/shard_map/scatter-add | solution.py:150
  647.9 14.7 %all-reduce.12 = (f32[]{:T(128)}, f32[]{:T(128)}) all-reduce(f32[]{:T(128)} %get-tuple-element.32, f32[]{:T(128)} %get-tuple-element.31), channel_id=1, replica_groups=mesh['gx'=4,'gy_0'=4,'gy_1'=2,'gz_0'=4,'gz_1'=4] {'gx'}, use_global_device_ids=true, to_apply=%region_58.59 | all-reduce | flops 2 | bytes 16 | tf_op jit(solution)/shard_map/psum | solution.py:16
  662.6 10.1 %all-reduce.8 = (f32[]{:T(128)}, f32[]{:T(128)}) all-reduce(f32[]{:T(128)} %get-tuple-element.79, f32[]{:T(128)} %get-tuple-element.80), channel_id=1, replica_groups=mesh['gx'=4,'gy_0'=4,'gy_1'=2,'gz_0'=4,'gz_1'=4] {'gy_0'}, use_global_device_ids=true, to_apply=%region_59.60 | all-reduce | flops 2 | bytes 16 | tf_op jit(solution)/shard_map/psum | solution.py:16
  684.2 13.5 %all-reduce = (f32[]{:T(128)}, f32[]{:T(128)}) all-reduce(f32[]{:T(128)} %get-tuple-element.63, f32[]{:T(128)} %get-tuple-element.64), channel_id=1, replica_groups=mesh['gx'=4,'gy_0'=4,'gy_1'=2,'gz_0'=4,'gz_1'=4] {'gz_1'}, use_global_device_ids=true, to_apply=%region_62.63 | all-reduce | flops 2 | bytes 16 | tf_op jit(solution)/shard_map/psum | solution.py:16
  (336 shorter events, 346.8 us)
Async XLA Ops:
  2.9 59.4 %collective-permute-start.7 = (s32[1,1,1,3,832]{4,3,2,1,0:T(4,128)S(1)}, s32[1,1,1,3,832]{4,3,2,1,0:T(4,128)S(1)}, u32[]{:S(2)}, u32[]{:S(2)}) collective-permute-start(s32[1,1,1,3,832]{4,3,2,1,0:T(4,128)S(1)} %add_bitcast_fusion.1), channel_id=1, source_target_pairs={{128,0},{256,128},{384,256},{0,384},{129,1},{257,129},{385,257},{1... | collective-permute-start | bytes 29960 | tf_op jit(solution)/shard_map/ppermute | solution.py:29
  15.7 47.1 %collective-permute-start.6 = (s32[1,1,1,3,832]{4,3,2,1,0:T(4,128)S(1)}, s32[1,1,1,3,832]{4,3,2,1,0:T(4,128)S(1)}, u32[]{:S(2)}, u32[]{:S(2)}) collective-permute-start(s32[1,1,1,3,832]{4,3,2,1,0:T(4,128)S(1)} %add_bitcast_fusion.1), channel_id=1, source_target_pairs={{0,128},{128,256},{256,384},{384,0},{1,129},{129,257},{257,385},{3... | collective-permute-start | bytes 29960 | tf_op jit(solution)/shard_map/ppermute | solution.py:26
  18.4 43.9 %collective-permute-start.1 = (f32[1,1,1,6,256]{4,3,2,1,0:T(8,128)S(1)}, f32[1,1,1,6,256]{4,3,2,1,0:T(8,128)S(1)}, u32[]{:S(2)}, u32[]{:S(2)}) collective-permute-start(f32[1,1,1,6,256]{4,3,2,1,0:T(8,128)S(1)} %slice_bitcast_fusion.5), channel_id=1, source_target_pairs={{128,0},{256,128},{384,256},{0,384},{129,1},{257,129},{385,257},{1... | collective-permute-start | bytes 18440 | tf_op jit(solution)/shard_map/ppermute | solution.py:29
  26.2 34.1 %collective-permute-start = (f32[1,1,1,6,256]{4,3,2,1,0:T(8,128)S(1)}, f32[1,1,1,6,256]{4,3,2,1,0:T(8,128)S(1)}, u32[]{:S(2)}, u32[]{:S(2)}) collective-permute-start(f32[1,1,1,6,256]{4,3,2,1,0:T(8,128)S(1)} %slice_bitcast_fusion.5), channel_id=1, source_target_pairs={{0,128},{128,256},{256,384},{384,0},{1,129},{129,257},{257,385},{3... | collective-permute-start | bytes 18440 | tf_op jit(solution)/shard_map/ppermute | solution.py:26
  29.8 40.5 %collective-permute-start.13 = (f32[1,1,1,5,832]{4,3,2,1,0:T(8,128)S(1)}, f32[1,1,1,5,832]{4,3,2,1,0:T(8,128)S(1)}, u32[]{:S(2)}, u32[]{:S(2)}) collective-permute-start(f32[1,1,1,5,832]{4,3,2,1,0:T(8,128)S(1)} %maximum_bitcast_fusion.4), channel_id=1, source_target_pairs={{128,0},{256,128},{384,256},{0,384},{129,1},{257,129},{385,257},{1... | collective-permute-start | bytes 49928 | tf_op jit(solution)/shard_map/ppermute | solution.py:29
  60.3 10.0 %collective-permute-start.12 = (f32[1,1,1,5,832]{4,3,2,1,0:T(8,128)S(1)}, f32[1,1,1,5,832]{4,3,2,1,0:T(8,128)S(1)}, u32[]{:S(2)}, u32[]{:S(2)}) collective-permute-start(f32[1,1,1,5,832]{4,3,2,1,0:T(8,128)S(1)} %maximum_bitcast_fusion.4), channel_id=1, source_target_pairs={{0,128},{128,256},{256,384},{384,0},{1,129},{129,257},{257,385},{3... | collective-permute-start | bytes 49928 | tf_op jit(solution)/shard_map/ppermute | solution.py:26
  62.3 9.8 %collective-permute-start.3 = (f32[3,1,1,6,256]{4,2,3,1,0:T(1,128)S(1)}, f32[3,1,1,6,256]{4,2,3,1,0:T(1,128)S(1)}, u32[]{:S(2)}, u32[]{:S(2)}) collective-permute-start(f32[3,1,1,6,256]{4,2,3,1,0:T(1,128)S(1)} %constant_dynamic-update-slice_fusion), channel_id=1, source_target_pairs={{16,0},{32,16},{48,32},{64,48},{80,64},{96,80},{112,96},{0,112},{1... | collective-permute-start | bytes 55304 | tf_op jit(solution)/shard_map/ppermute | solution.py:29
  62.3 9.8 %collective-permute-start.2 = (f32[3,1,1,6,256]{4,2,3,1,0:T(1,128)S(1)}, f32[3,1,1,6,256]{4,2,3,1,0:T(1,128)S(1)}, u32[]{:S(2)}, u32[]{:S(2)}) collective-permute-start(f32[3,1,1,6,256]{4,2,3,1,0:T(1,128)S(1)} %constant_dynamic-update-slice_fusion), channel_id=1, source_target_pairs={{0,16},{16,32},{32,48},{48,64},{64,80},{80,96},{96,112},{112,0},{1... | collective-permute-start | bytes 55304 | tf_op jit(solution)/shard_map/ppermute | solution.py:26
  62.8 15.1 %collective-permute-start.9 = (s32[3,1,1,3,832]{4,3,2,1,0:T(4,128)S(1)}, s32[3,1,1,3,832]{4,3,2,1,0:T(4,128)S(1)}, u32[]{:S(2)}, u32[]{:S(2)}) collective-permute-start(s32[3,1,1,3,832]{4,3,2,1,0:T(4,128)S(1)} %pad_add_fusion.2), channel_id=1, source_target_pairs={{16,0},{32,16},{48,32},{64,48},{80,64},{96,80},{112,96},{0,112},{1... | collective-permute-start | bytes 89864 | tf_op jit(solution)/shard_map/ppermute | solution.py:29
  70.4 17.4 %collective-permute-start.15 = (f32[3,1,1,5,832]{4,2,3,1,0:T(1,128)S(1)}, f32[3,1,1,5,832]{4,2,3,1,0:T(1,128)S(1)}, u32[]{:S(2)}, u32[]{:S(2)}) collective-permute-start(f32[3,1,1,5,832]{4,2,3,1,0:T(1,128)S(1)} %constant_dynamic-update-slice_fusion.3), channel_id=1, source_target_pairs={{16,0},{32,16},{48,32},{64,48},{80,64},{96,80},{112,96},{0,112},{1... | collective-permute-start | bytes 149768 | tf_op jit(solution)/shard_map/ppermute | solution.py:29
  72.1 17.6 %collective-permute-start.14 = (f32[3,1,1,5,832]{4,2,3,1,0:T(1,128)S(1)}, f32[3,1,1,5,832]{4,2,3,1,0:T(1,128)S(1)}, u32[]{:S(2)}, u32[]{:S(2)}) collective-permute-start(f32[3,1,1,5,832]{4,2,3,1,0:T(1,128)S(1)} %constant_dynamic-update-slice_fusion.3), channel_id=1, source_target_pairs={{0,16},{16,32},{32,48},{48,64},{64,80},{80,96},{96,112},{112,0},{1... | collective-permute-start | bytes 149768 | tf_op jit(solution)/shard_map/ppermute | solution.py:26
  72.2 26.2 %collective-permute-start.5 = (f32[3,3,1,6,256]{4,2,3,1,0:T(1,128)S(1)}, f32[3,3,1,6,256]{4,2,3,1,0:T(1,128)S(1)}, u32[]{:S(2)}, u32[]{:S(2)}) collective-permute-start(f32[3,3,1,6,256]{4,2,3,1,0:T(1,128)S(1)} %pad_maximum_fusion.6), channel_id=1, source_target_pairs={{1,0},{2,1},{3,2},{4,3},{5,4},{6,5},{7,6},{8,7},{9,8},{10,9},{11,1... | collective-permute-start | bytes 165896 | tf_op jit(solution)/shard_map/ppermute | solution.py:29
  77.9 22.4 %collective-permute-start.4 = (f32[3,3,1,6,256]{4,2,3,1,0:T(1,128)S(1)}, f32[3,3,1,6,256]{4,2,3,1,0:T(1,128)S(1)}, u32[]{:S(2)}, u32[]{:S(2)}) collective-permute-start(f32[3,3,1,6,256]{4,2,3,1,0:T(1,128)S(1)} %pad_maximum_fusion.6), channel_id=1, source_target_pairs={{0,1},{1,2},{2,3},{3,4},{4,5},{5,6},{6,7},{7,8},{8,9},{9,10},{10,1... | collective-permute-start | bytes 165896 | tf_op jit(solution)/shard_map/ppermute | solution.py:26
  79.9 72.3 %collective-permute-start.11 = (s32[3,3,1,3,832]{4,3,2,1,0:T(4,128)S(1)}, s32[3,3,1,3,832]{4,3,2,1,0:T(4,128)}, u32[]{:S(2)}, u32[]{:S(2)}) collective-permute-start(s32[3,3,1,3,832]{4,3,2,1,0:T(4,128)S(1)} %pad_add_fusion.1), channel_id=1, source_target_pairs={{1,0},{2,1},{3,2},{4,3},{5,4},{6,5},{7,6},{8,7},{9,8},{10,9},{11,1... | collective-permute-start | bytes 269576 | tf_op jit(solution)/shard_map/ppermute | solution.py:29
  87.8 64.4 %collective-permute-start.10 = (s32[3,3,1,3,832]{4,3,2,1,0:T(4,128)S(1)}, s32[3,3,1,3,832]{4,3,2,1,0:T(4,128)}, u32[]{:S(2)}, u32[]{:S(2)}) collective-permute-start(s32[3,3,1,3,832]{4,3,2,1,0:T(4,128)S(1)} %pad_add_fusion.1), channel_id=1, source_target_pairs={{0,1},{1,2},{2,3},{3,4},{4,5},{5,6},{6,7},{7,8},{8,9},{9,10},{10,1... | collective-permute-start | bytes 269576 | tf_op jit(solution)/shard_map/ppermute | solution.py:26
  90.5 74.3 %collective-permute-start.17 = (f32[3,3,1,5,832]{4,2,3,1,0:T(1,128)}, f32[3,3,1,5,832]{4,2,3,1,0:T(1,128)}, u32[]{:S(2)}, u32[]{:S(2)}) collective-permute-start(f32[3,3,1,5,832]{4,2,3,1,0:T(1,128)} %pad_maximum_fusion.5), channel_id=1, source_target_pairs={{1,0},{2,1},{3,2},{4,3},{5,4},{6,5},{7,6},{8,7},{9,8},{10,9},{11,1... | collective-permute-start | bytes 449288 | tf_op jit(solution)/shard_map/ppermute | solution.py:29
  98.3 66.5 %collective-permute-start.16 = (f32[3,3,1,5,832]{4,2,3,1,0:T(1,128)}, f32[3,3,1,5,832]{4,2,3,1,0:T(1,128)}, u32[]{:S(2)}, u32[]{:S(2)}) collective-permute-start(f32[3,3,1,5,832]{4,2,3,1,0:T(1,128)} %pad_maximum_fusion.5), channel_id=1, source_target_pairs={{0,1},{1,2},{2,3},{3,4},{4,5},{5,6},{6,7},{7,8},{8,9},{9,10},{10,1... | collective-permute-start | bytes 449288 | tf_op jit(solution)/shard_map/ppermute | solution.py:26
  235.8 9.8 %collective-permute-start.18 = (f32[1,1,1,6,256]{4,3,2,1,0:T(8,128)S(1)}, f32[1,1,1,6,256]{4,3,2,1,0:T(8,128)S(1)}, u32[]{:S(2)}, u32[]{:S(2)}) collective-permute-start(f32[1,1,1,6,256]{4,3,2,1,0:T(8,128)S(1)} %slice_bitcast_fusion.4), channel_id=1, source_target_pairs={{0,128},{128,256},{256,384},{384,0},{1,129},{129,257},{257,385},{3... | collective-permute-start | bytes 18440 | tf_op jit(solution)/shard_map/ppermute | solution.py:26
  259.0 16.8 %collective-permute-start.23 = (f32[3,3,1,6,256]{4,2,3,1,0:T(1,128)S(1)}, f32[3,3,1,6,256]{4,2,3,1,0:T(1,128)S(1)}, u32[]{:S(2)}, u32[]{:S(2)}) collective-permute-start(f32[3,3,1,6,256]{4,2,3,1,0:T(1,128)S(1)} %pad_maximum_fusion.7), channel_id=1, source_target_pairs={{1,0},{2,1},{3,2},{4,3},{5,4},{6,5},{7,6},{8,7},{9,8},{10,9},{11,1... | collective-permute-start | bytes 165896 | tf_op jit(solution)/shard_map/ppermute | solution.py:29
  260.9 14.9 %collective-permute-start.22 = (f32[3,3,1,6,256]{4,2,3,1,0:T(1,128)S(1)}, f32[3,3,1,6,256]{4,2,3,1,0:T(1,128)S(1)}, u32[]{:S(2)}, u32[]{:S(2)}) collective-permute-start(f32[3,3,1,6,256]{4,2,3,1,0:T(1,128)S(1)} %pad_maximum_fusion.7), channel_id=1, source_target_pairs={{0,1},{1,2},{2,3},{3,4},{4,5},{5,6},{6,7},{7,8},{8,9},{9,10},{10,1... | collective-permute-start | bytes 165896 | tf_op jit(solution)/shard_map/ppermute | solution.py:26
  415.4 17.0 %collective-permute-start.29 = (f32[3,3,1,6,256]{4,2,3,1,0:T(1,128)S(1)}, f32[3,3,1,6,256]{4,2,3,1,0:T(1,128)S(1)}, u32[]{:S(2)}, u32[]{:S(2)}) collective-permute-start(f32[3,3,1,6,256]{4,2,3,1,0:T(1,128)S(1)} %pad_maximum_fusion.8), channel_id=1, source_target_pairs={{1,0},{2,1},{3,2},{4,3},{5,4},{6,5},{7,6},{8,7},{9,8},{10,9},{11,1... | collective-permute-start | bytes 165896 | tf_op jit(solution)/shard_map/ppermute | solution.py:29
  417.3 15.1 %collective-permute-start.28 = (f32[3,3,1,6,256]{4,2,3,1,0:T(1,128)S(1)}, f32[3,3,1,6,256]{4,2,3,1,0:T(1,128)S(1)}, u32[]{:S(2)}, u32[]{:S(2)}) collective-permute-start(f32[3,3,1,6,256]{4,2,3,1,0:T(1,128)S(1)} %pad_maximum_fusion.8), channel_id=1, source_target_pairs={{0,1},{1,2},{2,3},{3,4},{4,5},{5,6},{6,7},{7,8},{8,9},{9,10},{10,1... | collective-permute-start | bytes 165896 | tf_op jit(solution)/shard_map/ppermute | solution.py:26
  569.3 16.8 %collective-permute-start.35 = (f32[3,3,1,6,256]{4,2,3,1,0:T(1,128)S(1)}, f32[3,3,1,6,256]{4,2,3,1,0:T(1,128)S(1)}, u32[]{:S(2)}, u32[]{:S(2)}) collective-permute-start(f32[3,3,1,6,256]{4,2,3,1,0:T(1,128)S(1)} %pad_maximum_fusion.9), channel_id=1, source_target_pairs={{1,0},{2,1},{3,2},{4,3},{5,4},{6,5},{7,6},{8,7},{9,8},{10,9},{11,1... | collective-permute-start | bytes 165896 | tf_op jit(solution)/shard_map/ppermute | solution.py:29
  571.2 14.9 %collective-permute-start.34 = (f32[3,3,1,6,256]{4,2,3,1,0:T(1,128)S(1)}, f32[3,3,1,6,256]{4,2,3,1,0:T(1,128)S(1)}, u32[]{:S(2)}, u32[]{:S(2)}) collective-permute-start(f32[3,3,1,6,256]{4,2,3,1,0:T(1,128)S(1)} %pad_maximum_fusion.9), channel_id=1, source_target_pairs={{0,1},{1,2},{2,3},{3,4},{4,5},{5,6},{6,7},{7,8},{8,9},{9,10},{10,1... | collective-permute-start | bytes 165896 | tf_op jit(solution)/shard_map/ppermute | solution.py:26
  (18 other events, 160.6 us)
where the time goes:
time: 712 us; the launch traced here: 703 us
  blocking collectives  199 us (28%)
  other arithmetic  180 us (25%)
  local copies, waits for them, and re-layouts  176 us (25%)
  starting transfers between devices  114 us (16%)
  waiting for transfers between devices  18 us (3%)
  between operations  16.3 us (2%)
    psum x20, blocking collectives, one_axis_at_a_time(): value = lax.psum(value, axis)  199 us
    ppermute x18, starting transfers between devices, with_halo(): lax.ppermute(lax.slice_in_dim(block, 0, width, axis=dim), axis, backward)  75.1 us
    scatter-add x4, other arithmetic, operate(): forces.at[:, near_grain].add(jnp.where(far_slot[None], 0.0, on_second))  73.9 us
    scatter-add x4, other arithmetic, operate(): forces = jnp.zeros_like(field).at[:, owners].add(on_first)  68.5 us
    gather x8, local copies, waits for them, and re-layouts, operate(): rim_flat[:, ghost_column]  42.4 us
    ppermute x18, starting transfers between devices, with_halo(): lax.ppermute(lax.slice_in_dim(block, block.shape[dim] - width, None, axis...  38.9 us
    gather x8, local copies, waits for them, and re-layouts, operate(): field[:, near_grain]  34.5 us
    gather x8, local copies, waits for them, and re-layouts, operate(): first_u = field[:, owners]  34.4 us
  transfers between devices with their start and end apart: 36, of which 4 were waited for; matrix products, arithmetic and copies ran while one was open for 21% of the time, Pallas kernels for 0%

commit v1 on v0

--- a/solution.py
+++ b/solution.py
@@ -13,7 +13,7 @@
 
 def one_axis_at_a_time(value, axes):
     for axis in axes:
-        value = lax.psum(value, axis)
+        value = jnp.sum(lax.all_gather(value, axis), axis=0)
     return value
 
 

time: 712 us -> 789 us (1.11)
  local copies, waits for them, and re-layouts: 176 us -> 240 us
  other arithmetic: 180 us -> 206 us
  blocking collectives: 199 us -> 186 us
    psum x20 -> x0, blocking collectives: 199 us -> none  [one_axis_at_a_time(): value = lax.psum(value, axis)]
    unnamed x0 -> x20, blocking collectives: none -> 186 us
    unnamed x27 -> x112, local copies, waits for them, and re-layouts: 3.93 us -> 64.8 us
    reduce_sum x0 -> x40, other arithmetic: none -> 24.4 us  [one_axis_at_a_time(): value = jnp.sum(lax.all_gather(value, axis), axis=0)]
  transfers between devices with their start and end apart: 36 -> 36, of which waited for: 4 -> 4; matrix products, arithmetic and copies ran while one was open for 21% -> 19% of each run, Pallas kernels for 0% -> 0%
where the time goes in v1:
time: 789 us; the launch traced here: 779 us
  local copies, waits for them, and re-layouts  240 us (30%)
  other arithmetic  206 us (26%)
  blocking collectives  186 us (24%)
  starting transfers between devices  113 us (14%)
  waiting for transfers between devices  17.8 us (2%)
  between operations  16.4 us (2%)
    unnamed x20, blocking collectives  186 us
    ppermute x18, starting transfers between devices, with_halo(): lax.ppermute(lax.slice_in_dim(block, 0, width, axis=dim), axis, backward)  75.3 us
    scatter-add x4, other arithmetic, operate(): forces.at[:, near_grain].add(jnp.where(far_slot[None], 0.0, on_second))  73.9 us
    scatter-add x4, other arithmetic, operate(): forces = jnp.zeros_like(field).at[:, owners].add(on_first)  69.5 us
    unnamed x112, local copies, waits for them, and re-layouts  64.8 us
    gather x8, local copies, waits for them, and re-layouts, operate(): rim_flat[:, ghost_column]  42.4 us
    ppermute x18, starting transfers between devices, with_halo(): lax.ppermute(lax.slice_in_dim(block, block.shape[dim] - width, None, axis...  38.1 us
    gather x8, local copies, waits for them, and re-layouts, operate(): field[:, near_grain]  34.5 us
  transfers between devices with their start and end apart: 36, of which 4 were waited for; matrix products, arithmetic and copies ran while one was open for 19% of the time, Pallas kernels for 0%

profile of v1, /device:TPU:8, one launch (start us, length us, event | category | flops | bytes accessed | tf_op | source)
XLA Modules:
  0.0 779.4 jit_solution(7157268419755140640)
XLA Ops:
  2.9 12.7 %collective-permute-start.7 = (s32[1,1,1,3,832]{4,3,2,1,0:T(4,128)S(1)}, s32[1,1,1,3,832]{4,3,2,1,0:T(4,128)S(1)}, u32[]{:S(2)}, u32[]{:S(2)}) collective-permute-start(s32[1,1,1,3,832]{4,3,2,1,0:T(4,128)S(1)} %add_bitcast_fusion.1), channel_id=1, source_target_pairs={{128,0},{256,128},{384,256},{0,384},{129,1},{257,129},{385,257},{1... | collective-permute-start | bytes 29960 | tf_op jit(solution)/shard_map/ppermute | solution.py:29
  104.1 10.1 %gather_fusion = f32[3072,6]{1,0:T(8,128)S(1)} fusion(f32[6,6912]{0,1:T(8,128)} %bitcast.498, s32[3072]{0:T(1024)S(1)} %broadcast_clamp_fusion.2), kind=kCustom, calls=%fused_computation | custom fusion | bytes 159744 | tf_op jit(solution)/shard_map/gather | solution.py:147
  117.5 17.4 %scatter_custom_fusion = f32[6,1024]{0,1:T(8,128)S(1)} fusion(s32[3072]{0:T(1024)S(1)} %bitcast.594, f32[3072,6]{1,0:T(8,128)} %copy.972, f32[]{:T(128)} %constant.32.clone.1), kind=kCustom, calls=%fused_computation.42 | custom fusion | flops 18432 | bytes 25088 | tf_op jit(solution)/shard_map/scatter-add | solution.py:149
  134.9 18.6 %scatter_fusion = f32[6,1024]{0,1:T(8,128)S(1)} fusion(f32[6,1024]{0,1:T(8,128)S(1)} %scatter_custom_fusion, s32[3072]{0:T(1024)S(1)} %bitcast.539, f32[3072,6]{1,0:T(8,128)S(1)} %copy.973), kind=kCustom, calls=%fused_computation.23 | custom fusion | flops 18432 | bytes 233472 | tf_op jit(solution)/shard_map/scatter-add | solution.py:150
  188.5 13.9 %all-reduce.55 = (f32[4]{0:T(128)S(1)}, f32[4]{0:T(128)S(1)}) all-reduce(f32[4]{0:T(128)S(1)} %dynamic-update-slice, f32[4]{0:T(128)S(1)} %dynamic-update-slice.5), channel_id=1, replica_groups=mesh['gx'=4,'gy_0'=4,'gy_1'=2,'gz_0'=4,'gz_1'=4] {'gx'}, use_global_device_ids=true, to_apply=%add | all-reduce | flops 8 | bytes 64
  207.8 9.3 %all-reduce.51 = (f32[4]{0:T(128)S(1)}, f32[4]{0:T(128)S(1)}) all-reduce(f32[4]{0:T(128)S(1)} %dynamic-update-slice.1, f32[4]{0:T(128)S(1)} %dynamic-update-slice.6), channel_id=1, replica_groups=mesh['gx'=4,'gy_0'=4,'gy_1'=2,'gz_0'=4,'gz_1'=4] {'gy_0'}, use_global_device_ids=true, to_apply=%add.1 | all-reduce | flops 8 | bytes 64
  241.1 14.8 %all-reduce.43 = (f32[4]{0:T(128)S(1)}, f32[4]{0:T(128)S(1)}) all-reduce(f32[4]{0:T(128)S(1)} %dynamic-update-slice.4, f32[4]{0:T(128)S(1)} %dynamic-update-slice.9), channel_id=1, replica_groups=mesh['gx'=4,'gy_0'=4,'gy_1'=2,'gz_0'=4,'gz_1'=4] {'gz_1'}, use_global_device_ids=true, to_apply=%add.4 | all-reduce | flops 8 | bytes 64
  304.6 10.1 %gather_fusion.7 = f32[3072,6]{1,0:T(8,128)S(1)} fusion(f32[6,6912]{0,1:T(8,128)} %bitcast.503, s32[3072]{0:T(1024)S(1)} %broadcast_clamp_fusion.2), kind=kCustom, calls=%fused_computation.7 | custom fusion | bytes 159744 | tf_op jit(solution)/shard_map/gather | solution.py:147
  318.7 17.4 %scatter_custom_fusion.3 = f32[6,1024]{0,1:T(8,128)S(1)} fusion(s32[3072]{0:T(1024)S(1)} %bitcast.595, f32[3072,6]{1,0:T(8,128)} %copy.998, f32[]{:T(128)} %constant.32.clone.1), kind=kCustom, calls=%fused_computation.40 | custom fusion | flops 18432 | bytes 25088 | tf_op jit(solution)/shard_map/scatter-add | solution.py:149
  336.0 18.4 %scatter_fusion.2 = f32[6,1024]{0,1:T(8,128)S(1)} fusion(f32[6,1024]{0,1:T(8,128)S(1)} %scatter_custom_fusion.3, s32[3072]{0:T(1024)S(1)} %bitcast.540, f32[3072,6]{1,0:T(8,128)S(1)} %copy.999), kind=kCustom, calls=%fused_computation.26 | custom fusion | flops 18432 | bytes 233472 | tf_op jit(solution)/shard_map/scatter-add | solution.py:150
  364.5 14.0 %all-reduce.54 = (f32[4]{0:T(128)S(1)}, f32[4]{0:T(128)S(1)}) all-reduce(f32[4]{0:T(128)S(1)} %dynamic-update-slice.10, f32[4]{0:T(128)S(1)} %dynamic-update-slice.15), channel_id=1, replica_groups=mesh['gx'=4,'gy_0'=4,'gy_1'=2,'gz_0'=4,'gz_1'=4] {'gx'}, use_global_device_ids=true, to_apply=%add.10 | all-reduce | flops 8 | bytes 64
  382.4 9.5 %all-reduce.50 = (f32[4]{0:T(128)S(1)}, f32[4]{0:T(128)S(1)}) all-reduce(f32[4]{0:T(128)S(1)} %dynamic-update-slice.11, f32[4]{0:T(128)S(1)} %dynamic-update-slice.16), channel_id=1, replica_groups=mesh['gx'=4,'gy_0'=4,'gy_1'=2,'gz_0'=4,'gz_1'=4] {'gy_0'}, use_global_device_ids=true, to_apply=%add.11 | all-reduce | flops 8 | bytes 64
  413.9 12.8 %all-reduce.42 = (f32[4]{0:T(128)S(1)}, f32[4]{0:T(128)S(1)}) all-reduce(f32[4]{0:T(128)S(1)} %dynamic-update-slice.14, f32[4]{0:T(128)S(1)} %dynamic-update-slice.19), channel_id=1, replica_groups=mesh['gx'=4,'gy_0'=4,'gy_1'=2,'gz_0'=4,'gz_1'=4] {'gz_1'}, use_global_device_ids=true, to_apply=%add.14 | all-reduce | flops 8 | bytes 64
  478.7 10.1 %gather_fusion.12 = f32[3072,6]{1,0:T(8,128)S(1)} fusion(f32[6,6912]{0,1:T(8,128)} %bitcast.505, s32[3072]{0:T(1024)S(1)} %broadcast_clamp_fusion.2), kind=kCustom, calls=%fused_computation.12 | custom fusion | bytes 159744 | tf_op jit(solution)/shard_map/gather | solution.py:147
  492.8 17.4 %scatter_custom_fusion.6 = f32[6,1024]{0,1:T(8,128)S(1)} fusion(s32[3072]{0:T(1024)S(1)} %bitcast.596, f32[3072,6]{1,0:T(8,128)} %copy.1017, f32[]{:T(128)} %constant.32.clone.1), kind=kCustom, calls=%fused_computation.38 | custom fusion | flops 18432 | bytes 25088 | tf_op jit(solution)/shard_map/scatter-add | solution.py:149
  510.2 18.4 %scatter_fusion.4 = f32[6,1024]{0,1:T(8,128)S(1)} fusion(f32[6,1024]{0,1:T(8,128)S(1)} %scatter_custom_fusion.6, s32[3072]{0:T(1024)S(1)} %bitcast.541, f32[3072,6]{1,0:T(8,128)S(1)} %copy.1018), kind=kCustom, calls=%fused_computation.29 | custom fusion | flops 18432 | bytes 233472 | tf_op jit(solution)/shard_map/scatter-add | solution.py:150
  538.5 14.0 %all-reduce.53 = (f32[4]{0:T(128)S(1)}, f32[4]{0:T(128)S(1)}) all-reduce(f32[4]{0:T(128)S(1)} %dynamic-update-slice.20, f32[4]{0:T(128)S(1)} %dynamic-update-slice.25), channel_id=1, replica_groups=mesh['gx'=4,'gy_0'=4,'gy_1'=2,'gz_0'=4,'gz_1'=4] {'gx'}, use_global_device_ids=true, to_apply=%add.20 | all-reduce | flops 8 | bytes 64
  586.4 12.7 %all-reduce.41 = (f32[4]{0:T(128)S(1)}, f32[4]{0:T(128)S(1)}) all-reduce(f32[4]{0:T(128)S(1)} %dynamic-update-slice.24, f32[4]{0:T(128)S(1)} %dynamic-update-slice.29), channel_id=1, replica_groups=mesh['gx'=4,'gy_0'=4,'gy_1'=2,'gz_0'=4,'gz_1'=4] {'gz_1'}, use_global_device_ids=true, to_apply=%add.24 | all-reduce | flops 8 | bytes 64
  650.5 10.1 %gather_fusion.17 = f32[3072,6]{1,0:T(8,128)S(1)} fusion(f32[6,6912]{0,1:T(8,128)} %bitcast.501, s32[3072]{0:T(1024)S(1)} %broadcast_clamp_fusion.2), kind=kCustom, calls=%fused_computation.17 | custom fusion | bytes 159744 | tf_op jit(solution)/shard_map/gather | solution.py:147
  664.5 17.4 %scatter_custom_fusion.9 = f32[6,1024]{0,1:T(8,128)S(1)} fusion(s32[3072]{0:T(1024)S(1)} %bitcast.597, f32[3072,6]{1,0:T(8,128)} %copy.1036, f32[]{:T(128)} %constant.32.clone.1), kind=kCustom, calls=%fused_computation.36 | custom fusion | flops 18432 | bytes 25088 | tf_op jit(solution)/shard_map/scatter-add | solution.py:149
  681.9 18.4 %scatter_fusion.6 = f32[6,1024]{0,1:T(8,128)S(1)} fusion(f32[6,1024]{0,1:T(8,128)S(1)} %scatter_custom_fusion.9, s32[3072]{0:T(1024)S(1)} %bitcast.542, f32[3072,6]{1,0:T(8,128)S(1)} %copy.1037), kind=kCustom, calls=%fused_computation.32 | custom fusion | flops 18432 | bytes 233472 | tf_op jit(solution)/shard_map/scatter-add | solution.py:150
  710.5 14.0 %all-reduce.52 = (f32[4]{0:T(128)S(1)}, f32[4]{0:T(128)S(1)}) all-reduce(f32[4]{0:T(128)S(1)} %dynamic-update-slice.30, f32[4]{0:T(128)S(1)} %dynamic-update-slice.35), channel_id=1, replica_groups=mesh['gx'=4,'gy_0'=4,'gy_1'=2,'gz_0'=4,'gz_1'=4] {'gx'}, use_global_device_ids=true, to_apply=%add.30 | all-reduce | flops 8 | bytes 64
  728.7 9.5 %all-reduce.48 = (f32[4]{0:T(128)S(1)}, f32[4]{0:T(128)S(1)}) all-reduce(f32[4]{0:T(128)S(1)} %dynamic-update-slice.31, f32[4]{0:T(128)S(1)} %dynamic-update-slice.36), channel_id=1, replica_groups=mesh['gx'=4,'gy_0'=4,'gy_1'=2,'gz_0'=4,'gz_1'=4] {'gy_0'}, use_global_device_ids=true, to_apply=%add.31 | all-reduce | flops 8 | bytes 64
  759.9 12.8 %all-reduce.40 = (f32[4]{0:T(128)S(1)}, f32[4]{0:T(128)S(1)}) all-reduce(f32[4]{0:T(128)S(1)} %dynamic-update-slice.34, f32[4]{0:T(128)S(1)} %dynamic-update-slice.39), channel_id=1, replica_groups=mesh['gx'=4,'gy_0'=4,'gy_1'=2,'gz_0'=4,'gz_1'=4] {'gz_1'}, use_global_device_ids=true, to_apply=%add.34 | all-reduce | flops 8 | bytes 64
  (461 shorter events, 429.0 us)
Async XLA Ops:
  2.9 60.7 %collective-permute-start.7 = (s32[1,1,1,3,832]{4,3,2,1,0:T(4,128)S(1)}, s32[1,1,1,3,832]{4,3,2,1,0:T(4,128)S(1)}, u32[]{:S(2)}, u32[]{:S(2)}) collective-permute-start(s32[1,1,1,3,832]{4,3,2,1,0:T(4,128)S(1)} %add_bitcast_fusion.1), channel_id=1, source_target_pairs={{128,0},{256,128},{384,256},{0,384},{129,1},{257,129},{385,257},{1... | collective-permute-start | bytes 29960 | tf_op jit(solution)/shard_map/ppermute | solution.py:29
  15.7 48.5 %collective-permute-start.6 = (s32[1,1,1,3,832]{4,3,2,1,0:T(4,128)S(1)}, s32[1,1,1,3,832]{4,3,2,1,0:T(4,128)S(1)}, u32[]{:S(2)}, u32[]{:S(2)}) collective-permute-start(s32[1,1,1,3,832]{4,3,2,1,0:T(4,128)S(1)} %add_bitcast_fusion.1), channel_id=1, source_target_pairs={{0,128},{128,256},{256,384},{384,0},{1,129},{129,257},{257,385},{3... | collective-permute-start | bytes 29960 | tf_op jit(solution)/shard_map/ppermute | solution.py:26
  18.4 45.2 %collective-permute-start.1 = (f32[1,1,1,6,256]{4,3,2,1,0:T(8,128)S(1)}, f32[1,1,1,6,256]{4,3,2,1,0:T(8,128)S(1)}, u32[]{:S(2)}, u32[]{:S(2)}) collective-permute-start(f32[1,1,1,6,256]{4,3,2,1,0:T(8,128)S(1)} %slice_bitcast_fusion.5), channel_id=1, source_target_pairs={{128,0},{256,128},{384,256},{0,384},{129,1},{257,129},{385,257},{1... | collective-permute-start | bytes 18440 | tf_op jit(solution)/shard_map/ppermute | solution.py:29
  26.2 35.4 %collective-permute-start = (f32[1,1,1,6,256]{4,3,2,1,0:T(8,128)S(1)}, f32[1,1,1,6,256]{4,3,2,1,0:T(8,128)S(1)}, u32[]{:S(2)}, u32[]{:S(2)}) collective-permute-start(f32[1,1,1,6,256]{4,3,2,1,0:T(8,128)S(1)} %slice_bitcast_fusion.5), channel_id=1, source_target_pairs={{0,128},{128,256},{256,384},{384,0},{1,129},{129,257},{257,385},{3... | collective-permute-start | bytes 18440 | tf_op jit(solution)/shard_map/ppermute | solution.py:26
  29.8 41.9 %collective-permute-start.13 = (f32[1,1,1,5,832]{4,3,2,1,0:T(8,128)S(1)}, f32[1,1,1,5,832]{4,3,2,1,0:T(8,128)S(1)}, u32[]{:S(2)}, u32[]{:S(2)}) collective-permute-start(f32[1,1,1,5,832]{4,3,2,1,0:T(8,128)S(1)} %maximum_bitcast_fusion.4), channel_id=1, source_target_pairs={{128,0},{256,128},{384,256},{0,384},{129,1},{257,129},{385,257},{1... | collective-permute-start | bytes 49928 | tf_op jit(solution)/shard_map/ppermute | solution.py:29
  61.6 10.0 %collective-permute-start.12 = (f32[1,1,1,5,832]{4,3,2,1,0:T(8,128)S(1)}, f32[1,1,1,5,832]{4,3,2,1,0:T(8,128)S(1)}, u32[]{:S(2)}, u32[]{:S(2)}) collective-permute-start(f32[1,1,1,5,832]{4,3,2,1,0:T(8,128)S(1)} %maximum_bitcast_fusion.4), channel_id=1, source_target_pairs={{0,128},{128,256},{256,384},{384,0},{1,129},{129,257},{257,385},{3... | collective-permute-start | bytes 49928 | tf_op jit(solution)/shard_map/ppermute | solution.py:26
  63.6 9.8 %collective-permute-start.3 = (f32[3,1,1,6,256]{4,2,3,1,0:T(1,128)S(1)}, f32[3,1,1,6,256]{4,2,3,1,0:T(1,128)S(1)}, u32[]{:S(2)}, u32[]{:S(2)}) collective-permute-start(f32[3,1,1,6,256]{4,2,3,1,0:T(1,128)S(1)} %constant_dynamic-update-slice_fusion), channel_id=1, source_target_pairs={{16,0},{32,16},{48,32},{64,48},{80,64},{96,80},{112,96},{0,112},{1... | collective-permute-start | bytes 55304 | tf_op jit(solution)/shard_map/ppermute | solution.py:29
  63.6 9.8 %collective-permute-start.2 = (f32[3,1,1,6,256]{4,2,3,1,0:T(1,128)S(1)}, f32[3,1,1,6,256]{4,2,3,1,0:T(1,128)S(1)}, u32[]{:S(2)}, u32[]{:S(2)}) collective-permute-start(f32[3,1,1,6,256]{4,2,3,1,0:T(1,128)S(1)} %constant_dynamic-update-slice_fusion), channel_id=1, source_target_pairs={{0,16},{16,32},{32,48},{48,64},{64,80},{80,96},{96,112},{112,0},{1... | collective-permute-start | bytes 55304 | tf_op jit(solution)/shard_map/ppermute | solution.py:26
  64.2 15.1 %collective-permute-start.9 = (s32[3,1,1,3,832]{4,3,2,1,0:T(4,128)S(1)}, s32[3,1,1,3,832]{4,3,2,1,0:T(4,128)S(1)}, u32[]{:S(2)}, u32[]{:S(2)}) collective-permute-start(s32[3,1,1,3,832]{4,3,2,1,0:T(4,128)S(1)} %pad_add_fusion.2), channel_id=1, source_target_pairs={{16,0},{32,16},{48,32},{64,48},{80,64},{96,80},{112,96},{0,112},{1... | collective-permute-start | bytes 89864 | tf_op jit(solution)/shard_map/ppermute | solution.py:29
  71.7 17.4 %collective-permute-start.15 = (f32[3,1,1,5,832]{4,2,3,1,0:T(1,128)S(1)}, f32[3,1,1,5,832]{4,2,3,1,0:T(1,128)S(1)}, u32[]{:S(2)}, u32[]{:S(2)}) collective-permute-start(f32[3,1,1,5,832]{4,2,3,1,0:T(1,128)S(1)} %constant_dynamic-update-slice_fusion.3), channel_id=1, source_target_pairs={{16,0},{32,16},{48,32},{64,48},{80,64},{96,80},{112,96},{0,112},{1... | collective-permute-start | bytes 149768 | tf_op jit(solution)/shard_map/ppermute | solution.py:29
  73.5 17.6 %collective-permute-start.14 = (f32[3,1,1,5,832]{4,2,3,1,0:T(1,128)S(1)}, f32[3,1,1,5,832]{4,2,3,1,0:T(1,128)S(1)}, u32[]{:S(2)}, u32[]{:S(2)}) collective-permute-start(f32[3,1,1,5,832]{4,2,3,1,0:T(1,128)S(1)} %constant_dynamic-update-slice_fusion.3), channel_id=1, source_target_pairs={{0,16},{16,32},{32,48},{48,64},{64,80},{80,96},{96,112},{112,0},{1... | collective-permute-start | bytes 149768 | tf_op jit(solution)/shard_map/ppermute | solution.py:26
  73.5 26.2 %collective-permute-start.5 = (f32[3,3,1,6,256]{4,2,3,1,0:T(1,128)S(1)}, f32[3,3,1,6,256]{4,2,3,1,0:T(1,128)S(1)}, u32[]{:S(2)}, u32[]{:S(2)}) collective-permute-start(f32[3,3,1,6,256]{4,2,3,1,0:T(1,128)S(1)} %pad_maximum_fusion.6), channel_id=1, source_target_pairs={{1,0},{2,1},{3,2},{4,3},{5,4},{6,5},{7,6},{8,7},{9,8},{10,9},{11,1... | collective-permute-start | bytes 165896 | tf_op jit(solution)/shard_map/ppermute | solution.py:29
  79.3 22.4 %collective-permute-start.4 = (f32[3,3,1,6,256]{4,2,3,1,0:T(1,128)S(1)}, f32[3,3,1,6,256]{4,2,3,1,0:T(1,128)S(1)}, u32[]{:S(2)}, u32[]{:S(2)}) collective-permute-start(f32[3,3,1,6,256]{4,2,3,1,0:T(1,128)S(1)} %pad_maximum_fusion.6), channel_id=1, source_target_pairs={{0,1},{1,2},{2,3},{3,4},{4,5},{5,6},{6,7},{7,8},{8,9},{9,10},{10,1... | collective-permute-start | bytes 165896 | tf_op jit(solution)/shard_map/ppermute | solution.py:26
  81.3 72.3 %collective-permute-start.11 = (s32[3,3,1,3,832]{4,3,2,1,0:T(4,128)S(1)}, s32[3,3,1,3,832]{4,3,2,1,0:T(4,128)}, u32[]{:S(2)}, u32[]{:S(2)}) collective-permute-start(s32[3,3,1,3,832]{4,3,2,1,0:T(4,128)S(1)} %pad_add_fusion.1), channel_id=1, source_target_pairs={{1,0},{2,1},{3,2},{4,3},{5,4},{6,5},{7,6},{8,7},{9,8},{10,9},{11,1... | collective-permute-start | bytes 269576 | tf_op jit(solution)/shard_map/ppermute | solution.py:29
  89.1 64.4 %collective-permute-start.10 = (s32[3,3,1,3,832]{4,3,2,1,0:T(4,128)S(1)}, s32[3,3,1,3,832]{4,3,2,1,0:T(4,128)}, u32[]{:S(2)}, u32[]{:S(2)}) collective-permute-start(s32[3,3,1,3,832]{4,3,2,1,0:T(4,128)S(1)} %pad_add_fusion.1), channel_id=1, source_target_pairs={{0,1},{1,2},{2,3},{3,4},{4,5},{5,6},{6,7},{7,8},{8,9},{9,10},{10,1... | collective-permute-start | bytes 269576 | tf_op jit(solution)/shard_map/ppermute | solution.py:26
  91.9 74.3 %collective-permute-start.17 = (f32[3,3,1,5,832]{4,2,3,1,0:T(1,128)}, f32[3,3,1,5,832]{4,2,3,1,0:T(1,128)}, u32[]{:S(2)}, u32[]{:S(2)}) collective-permute-start(f32[3,3,1,5,832]{4,2,3,1,0:T(1,128)} %pad_maximum_fusion.5), channel_id=1, source_target_pairs={{1,0},{2,1},{3,2},{4,3},{5,4},{6,5},{7,6},{8,7},{9,8},{10,9},{11,1... | collective-permute-start | bytes 449288 | tf_op jit(solution)/shard_map/ppermute | solution.py:29
  99.7 66.5 %collective-permute-start.16 = (f32[3,3,1,5,832]{4,2,3,1,0:T(1,128)}, f32[3,3,1,5,832]{4,2,3,1,0:T(1,128)}, u32[]{:S(2)}, u32[]{:S(2)}) collective-permute-start(f32[3,3,1,5,832]{4,2,3,1,0:T(1,128)} %pad_maximum_fusion.5), channel_id=1, source_target_pairs={{0,1},{1,2},{2,3},{3,4},{4,5},{5,6},{6,7},{7,8},{8,9},{9,10},{10,1... | collective-permute-start | bytes 449288 | tf_op jit(solution)/shard_map/ppermute | solution.py:26
  258.4 10.0 %collective-permute-start.18 = (f32[1,1,1,6,256]{4,3,2,1,0:T(8,128)S(1)}, f32[1,1,1,6,256]{4,3,2,1,0:T(8,128)S(1)}, u32[]{:S(2)}, u32[]{:S(2)}) collective-permute-start(f32[1,1,1,6,256]{4,3,2,1,0:T(8,128)S(1)} %slice_bitcast_fusion.4), channel_id=1, source_target_pairs={{0,128},{128,256},{256,384},{384,0},{1,129},{129,257},{257,385},{3... | collective-permute-start | bytes 18440 | tf_op jit(solution)/shard_map/ppermute | solution.py:26
  281.6 16.6 %collective-permute-start.23 = (f32[3,3,1,6,256]{4,2,3,1,0:T(1,128)S(1)}, f32[3,3,1,6,256]{4,2,3,1,0:T(1,128)S(1)}, u32[]{:S(2)}, u32[]{:S(2)}) collective-permute-start(f32[3,3,1,6,256]{4,2,3,1,0:T(1,128)S(1)} %pad_maximum_fusion.7), channel_id=1, source_target_pairs={{1,0},{2,1},{3,2},{4,3},{5,4},{6,5},{7,6},{8,7},{9,8},{10,9},{11,1... | collective-permute-start | bytes 165896 | tf_op jit(solution)/shard_map/ppermute | solution.py:29
  283.6 14.7 %collective-permute-start.22 = (f32[3,3,1,6,256]{4,2,3,1,0:T(1,128)S(1)}, f32[3,3,1,6,256]{4,2,3,1,0:T(1,128)S(1)}, u32[]{:S(2)}, u32[]{:S(2)}) collective-permute-start(f32[3,3,1,6,256]{4,2,3,1,0:T(1,128)S(1)} %pad_maximum_fusion.7), channel_id=1, source_target_pairs={{0,1},{1,2},{2,3},{3,4},{4,5},{5,6},{6,7},{7,8},{8,9},{9,10},{10,1... | collective-permute-start | bytes 165896 | tf_op jit(solution)/shard_map/ppermute | solution.py:26
  455.7 16.6 %collective-permute-start.29 = (f32[3,3,1,6,256]{4,2,3,1,0:T(1,128)S(1)}, f32[3,3,1,6,256]{4,2,3,1,0:T(1,128)S(1)}, u32[]{:S(2)}, u32[]{:S(2)}) collective-permute-start(f32[3,3,1,6,256]{4,2,3,1,0:T(1,128)S(1)} %pad_maximum_fusion.8), channel_id=1, source_target_pairs={{1,0},{2,1},{3,2},{4,3},{5,4},{6,5},{7,6},{8,7},{9,8},{10,9},{11,1... | collective-permute-start | bytes 165896 | tf_op jit(solution)/shard_map/ppermute | solution.py:29
  457.7 14.7 %collective-permute-start.28 = (f32[3,3,1,6,256]{4,2,3,1,0:T(1,128)S(1)}, f32[3,3,1,6,256]{4,2,3,1,0:T(1,128)S(1)}, u32[]{:S(2)}, u32[]{:S(2)}) collective-permute-start(f32[3,3,1,6,256]{4,2,3,1,0:T(1,128)S(1)} %pad_maximum_fusion.8), channel_id=1, source_target_pairs={{0,1},{1,2},{2,3},{3,4},{4,5},{5,6},{6,7},{7,8},{8,9},{9,10},{10,1... | collective-permute-start | bytes 165896 | tf_op jit(solution)/shard_map/ppermute | solution.py:26
  627.5 16.6 %collective-permute-start.35 = (f32[3,3,1,6,256]{4,2,3,1,0:T(1,128)S(1)}, f32[3,3,1,6,256]{4,2,3,1,0:T(1,128)S(1)}, u32[]{:S(2)}, u32[]{:S(2)}) collective-permute-start(f32[3,3,1,6,256]{4,2,3,1,0:T(1,128)S(1)} %pad_maximum_fusion.9), channel_id=1, source_target_pairs={{1,0},{2,1},{3,2},{4,3},{5,4},{6,5},{7,6},{8,7},{9,8},{10,9},{11,1... | collective-permute-start | bytes 165896 | tf_op jit(solution)/shard_map/ppermute | solution.py:29
  629.4 14.7 %collective-permute-start.34 = (f32[3,3,1,6,256]{4,2,3,1,0:T(1,128)S(1)}, f32[3,3,1,6,256]{4,2,3,1,0:T(1,128)S(1)}, u32[]{:S(2)}, u32[]{:S(2)}) collective-permute-start(f32[3,3,1,6,256]{4,2,3,1,0:T(1,128)S(1)} %pad_maximum_fusion.9), channel_id=1, source_target_pairs={{0,1},{1,2},{2,3},{3,4},{4,5},{5,6},{6,7},{7,8},{8,9},{9,10},{10,1... | collective-permute-start | bytes 165896 | tf_op jit(solution)/shard_map/ppermute | solution.py:26
  (18 other events, 160.6 us)
